TPU v7x, 32 devices: a whole 2x2x4 slice. The times are simulated.
32 devices in a mesh: dp: 32 (over z, y, x, core).
Axes of the slice: x: 2, y: 2, z: 4, core: 2. Of those that a mesh axis runs over, the one named last changes fastest.
Arguments:
- features: bfloat16 [32768, 3136], P('dp'), may hold values from -6 to 6
- w_one: bfloat16 [512, 3136], replicated, may hold values from -0.109375 to 0.109375
- b_one: float32 [512], replicated, may hold values from -3 to 3
- w_two: bfloat16 [512, 918], replicated, may hold values from -0.25 to 0.25
- b_two: float32 [918], replicated, may hold values from -112 to 112
- action: int32 [32768], P('dp'), may hold values from 0 to 17
- target_probs: float32 [32768, 18, 51], P('dp'), may hold values from 0 to 1, as said below
- next_action: int32 [32768], P('dp'), may hold values from 0 to 17
- lower_idx: int32 [32768, 51], P('dp'), may hold values from 0 to 49
- upper_frac: float32 [32768, 51], P('dp'), may hold values from 0 to 1
- is_weight: float32 [32768], P('dp'), may hold values from 0.1 to 1
Outputs:
- grad_w1: float32 [512, 3136], replicated
- grad_b1: float32 [512], replicated
- grad_w2: float32 [512, 918], replicated
- grad_b2: float32 [918], replicated
- mean_loss: float32 [], replicated
- priorities: float32 [32768], P('dp')
Inputs may be any that keep to these rules, and one draw needn't show every extreme that they name: Each target_probs[i, a] is a distribution over the atoms: positive entries that sum to one.
All inputs are finite; a program needn't handle non-finite values.
Results may differ from a plain program's by a relative error of at most 0.005.
Values sent between devices are 32-bit elements; how exact they have to be, the bound alone decides.
A program may use at most 128 MiB of HBM per device.

v0:
```python
import jax
import jax.numpy as jnp
from jax import lax
from jax.sharding import PartitionSpec as P


def forward_loss(
    features,
    w_one,
    b_one,
    w_two,
    b_two,
    action,
    target_probs,
    next_action,
    lower_idx,
    upper_frac,
    is_weight,
):
    row_count = features.shape[0]
    n_act = target_probs.shape[1]
    n_atom = target_probs.shape[2]
    pre_act = (
        lax.dot_general(
            features, w_one, (((1,), (1,)), ((), ())), preferred_element_type=jnp.float32
        )
        + b_one
    )
    hidden = jnp.maximum(pre_act, 0.0).astype(jnp.bfloat16)
    logits = (jnp.dot(hidden, w_two, preferred_element_type=jnp.float32) + b_two).reshape(
        row_count, n_act, n_atom
    )
    chosen = jnp.take_along_axis(logits, action[:, None, None], axis=1)[:, 0, :]
    log_probs = jax.nn.log_softmax(chosen, axis=-1)
    next_probs = jnp.take_along_axis(target_probs, next_action[:, None, None], axis=1)[:, 0, :]
    atom_ids = jnp.arange(n_atom, dtype=jnp.int32)
    mass_low = next_probs * (1.0 - upper_frac)
    mass_high = next_probs * upper_frac
    low_hot = lower_idx[:, :, None] == atom_ids[None, None, :]
    high_hot = lower_idx[:, :, None] + 1 == atom_ids[None, None, :]
    projected = jnp.sum(
        jnp.where(low_hot, mass_low[:, :, None], 0.0)
        + jnp.where(high_hot, mass_high[:, :, None], 0.0),
        axis=1,
    )
    cross_ent = -jnp.sum(projected * log_probs, axis=-1)
    grad_chosen = is_weight[:, None] * (
        jnp.exp(log_probs) * jnp.sum(projected, axis=-1, keepdims=True) - projected
    )
    act_hot = action[:, None] == jnp.arange(n_act, dtype=jnp.int32)[None, :]
    grad_logits = (
        jnp.where(act_hot[:, :, None], grad_chosen[:, None, :], 0.0)
        .reshape(row_count, n_act * n_atom)
        .astype(jnp.bfloat16)
    )
    grad_hidden = lax.dot_general(
        grad_logits, w_two, (((1,), (1,)), ((), ())), preferred_element_type=jnp.float32
    )
    grad_pre = jnp.where(pre_act > 0.0, grad_hidden, 0.0).astype(jnp.bfloat16)
    return (hidden, grad_logits, grad_pre, cross_ent)


def on_device(
    features,
    w_one,
    b_one,
    w_two,
    b_two,
    action,
    target_probs,
    next_action,
    lower_idx,
    upper_frac,
    is_weight,
):
    total_rows = features.shape[0] * lax.axis_size("dp")
    hidden, grad_logits, grad_pre, cross_ent = forward_loss(
        features,
        w_one,
        b_one,
        w_two,
        b_two,
        action,
        target_probs,
        next_action,
        lower_idx,
        upper_frac,
        is_weight,
    )
    local_loss = jnp.sum(is_weight * cross_ent)
    local_top = jnp.max(cross_ent)
    loss_sum = lax.psum(local_loss, "dp")
    top = lax.pmax(local_top, "dp")
    local_w2 = lax.dot_general(
        hidden, grad_logits, (((0,), (0,)), ((), ())), preferred_element_type=jnp.float32
    )
    local_b2 = jnp.sum(grad_logits.astype(jnp.float32), axis=0)
    local_b1 = jnp.sum(grad_pre.astype(jnp.float32), axis=0)
    grad_b1, grad_w2, grad_b2 = lax.psum((local_b1, local_w2, local_b2), "dp")
    local_w1 = lax.dot_general(
        grad_pre, features, (((0,), (0,)), ((), ())), preferred_element_type=jnp.float32
    )
    grad_w1 = lax.psum(local_w1, "dp")
    priorities = cross_ent / jnp.maximum(top, 1.0)
    mean_loss = loss_sum / total_rows
    return (grad_w1, grad_b1, grad_w2, grad_b2, mean_loss, priorities)


def solution(mesh):
    in_specs = (
        P("dp", None),
        P(),
        P(),
        P(),
        P(),
        P("dp"),
        P("dp", None, None),
        P("dp"),
        P("dp", None),
        P("dp", None),
        P("dp"),
    )
    out_specs = (P(), P(), P(), P(), P(), P("dp"))
    return jax.shard_map(
        on_device, mesh=mesh, in_specs=in_specs, out_specs=out_specs, check_vma=False
    )
```

profile of v0, /device:TPU:0, one launch (start us, length us, event | category | flops | bytes accessed | tf_op | source)
XLA Modules:
  0.0 283.7 jit_solution(31237595956415352)
XLA Ops:
  7.2 0.9 and_reduce_fusion
  8.1 0.8 iota_compare_fusion.2
  8.9 0.7 and_reduce_fusion.1
  9.6 1.0 broadcast_add_fusion
  10.6 5.9 %fusion.16 = f32[1024,512]{1,0:T(8,128)S(1)} fusion(bf16[1024,3136]{0,1:T(8,128)(2,1)} %param.13, bf16[512,3136]{0,1:T(8,128)(2,1)S(1)} %copy-done), kind=kOutput, calls=%fused_computation.50 | convolution fusion | flops 3288334336 | bytes 11730944 | tf_op jit(solution)/shard_map/dot_general | solution.py:24
  16.5 1.3 copy-done.10
  17.8 3.0 %convolution_add_fusion = f32[1024,918]{0,1:T(8,128)} fusion(bf16[512,918]{0,1:T(8,128)(2,1)S(1)} %copy-done.7, f32[918]{0:T(1024)S(1)} %copy-done.8, f32[1024,512]{1,0:T(8,128)S(1)} %fusion.16, f32[512]{0:T(512)S(1)} %copy-done.9), kind=kOutput, calls=%fused_computation.12 | convolution fusion | flops 965105664 | bytes 6803032 | tf_op jit(solution)/shard_map/dot_general | solution.py:30
  20.8 3.9 %reshape.118 = f32[1024,18,51]{0,2,1:T(8,128)} reshape(f32[1024,918]{0,1:T(8,128)} %convolution_add_fusion) | data formatting | bytes 7520256 | tf_op jit(solution)/shard_map/reshape | solution.py:30
  24.7 7.5 %copy.39 = f32[1024,18,51]{2,0,1:T(8,128)} copy(f32[1024,18,51]{0,2,1:T(8,128)} %reshape.118) | data formatting | bytes 7520256 | tf_op jit(solution)/shard_map/reshape | solution.py:30
  32.2 10.6 %gather_fusion = f32[1024,51]{1,0:T(8,128)S(1)} fusion(f32[1024,18,51]{2,0,1:T(8,128)} %copy.39, s32[1024]{0:T(1024)S(1)} %bitcast.54), kind=kCustom, calls=%fused_computation.clone | custom fusion | bytes 425984 | tf_op jit(solution)/shard_map/jit(take_along_axis)/gather | solution.py:33
  42.8 0.4 fusion.4
  43.2 0.5 exponential_reduce_fusion
  43.7 7.5 %copy.40 = f32[1024,18,51]{2,0,1:T(8,128)} copy(f32[1024,18,51]{0,2,1:T(8,128)} %param.19) | data formatting | bytes 7520256 | tf_op args[6]
  51.2 10.5 %gather_fusion.1 = f32[1024,51]{1,0:T(8,128)S(1)} fusion(f32[1024,18,51]{2,0,1:T(8,128)} %copy.40, s32[1024]{0:T(1024)S(1)} %bitcast.53), kind=kCustom, calls=%fused_computation.1.clone | custom fusion | bytes 425984 | tf_op jit(solution)/shard_map/jit(take_along_axis)/gather | solution.py:35
  61.7 0.2 copy.41
  62.0 4.5 %fusion.1 = (f32[1024]{0:T(1024)S(1)}, f32[1024,51]{0,1:T(8,128)S(1)}) fusion(f32[1024,51]{0,1:T(8,128)S(1)} %get-tuple-element.21, s32[1024,51]{0,1:T(8,128)S(1)} %broadcast_add_fusion, f32[1024,51]{0,1:T(8,128)S(1)} %get-tuple-element.20, s32[1024,51]{0,1:T(8,128)S(1)} %copy-done.4), kind=kLoop, calls=%fused_computation.5 | loop fusion | flops 18590720 | bytes 1048576 | tf_op jit(solution)/shard_map/reduce_sum | solution.py:48
  66.5 0.2 copy.42
  66.7 1.1 fusion.3
  67.9 0.4 select_convert_fusion
  68.3 1.8 convert_element_type.22
  70.1 3.9 %convert_reduce_fusion.1 = (f32[512]{0:T(512)S(1)}, bf16[1024,512]{1,0:T(8,128)(2,1)S(1)}) fusion(bf16[1024,918]{0,1:T(8,128)(2,1)} %convert_element_type.22, bf16[512,918]{0,1:T(8,128)(2,1)} %param.16, f32[1024,512]{1,0:T(8,128)} %copy-done.10, f32[512]{0:T(512)S(1)} %copy-done.9), kind=kOutput, calls=%fused_computation.9 | convolution fusion | flops 965737984 | bytes 5969920 | tf_op jit(solution)/shard_map/dot_general | solution.py:56
  74.1 2.4 fusion.5
  76.5 8.2 %fusion.17 = f32[512,3136]{0,1:T(8,128)} fusion(bf16[1024,3136]{0,1:T(8,128)(2,1)} %param.13, bf16[1024,512]{1,0:T(8,128)(2,1)S(1)} %get-tuple-element.25), kind=kOutput, calls=%fused_computation.51 | convolution fusion | flops 3288334336 | bytes 13893632 | tf_op jit(solution)/shard_map/dot_general | solution.py:100
  84.7 0.6 multiply_reduce_fusion
  85.3 0.6 negate_reduce_fusion
  85.9 43.8 %pmax.7 = f32[]{:T(128)} all-reduce(f32[]{:T(128)} %get-tuple-element.9), channel_id=1, replica_groups=mesh['dp'=32] {'dp'}, use_global_device_ids=true, to_apply=%region_14.16 | all-reduce | flops 1 | bytes 8 | tf_op jit(solution)/shard_map/pmax | solution.py:93
  129.7 0.5 convert_reduce_fusion
  131.0 41.0 %all-reduce = (f32[512]{0:T(512)}, f32[918]{0:T(1024)}, f32[]{:T(128)}) all-reduce(f32[512]{0:T(512)S(1)} %get-tuple-element.24, f32[918]{0:T(1024)S(1)} %reduce_sum.74, f32[]{:T(128)} %get-tuple-element.10), channel_id=1, replica_groups=mesh['dp'=32] {'dp'}, use_global_device_ids=true, to_apply=%region_6.8 | all-reduce | flops 1431 | bytes 11448 | tf_op jit(solution)/shard_map/psum | solution.py:99
  172.6 0.6 negate_divide_fusion
  173.2 94.7 %all-reduce.4.cloned.1.call-done = (f32[512,3136]{0,1:T(8,128)}, f32[512,918]{0,1:T(8,128)}) async-done(((f32[512,3136]{0,1:T(8,128)}, f32[512,918]{0,1:T(8,128)}), (f32[512,3136]{0,1:T(8,128)}, f32[512,918]{0,1:T(8,128)})) %all-reduce.4.cloned.1.call-update) | async-done | bytes 8302608 | tf_op jit(solution)/shard_map/psum | solution.py:103
  268.0 6.5 %copy.47 = f32[512,3136]{0,1:T(8,128)} copy(f32[512,3136]{0,1:T(8,128)} %get-tuple-element.28) | data formatting | bytes 12845056
  274.5 1.2 copy.48
  (32 shorter events, 0.5 us)
Async XLA Ops:
  7.2 3.4 %copy-start = (bf16[512,3136]{0,1:T(8,128)(2,1)S(1)}, bf16[512,3136]{0,1:T(8,128)(2,1)}, u32[]{:S(2)}) copy-start(bf16[512,3136]{0,1:T(8,128)(2,1)} %param.14) | copy-start | bytes 9633796
  7.2 260.8 %all-reduce.4.cloned.1.call-start = ((), (), s32[]{:S(2)}) async-start(), calls=%async_computation | async-start | bytes 16613376 | tf_op jit(solution)/shard_map/psum | solution.py:103
  10.5 7.3 %copy-start.7 = (bf16[512,918]{0,1:T(8,128)(2,1)S(1)}, bf16[512,918]{0,1:T(8,128)(2,1)}, u32[]{:S(2)}) copy-start(bf16[512,918]{0,1:T(8,128)(2,1)} %param.16) | copy-start | bytes 2820100
  10.6 7.3 %copy-start.8 = (f32[918]{0:T(1024)S(1)}, f32[918]{0:T(1024)}, u32[]{:S(2)}) copy-start(f32[918]{0:T(1024)} %param.17) | copy-start | bytes 11020
  10.6 7.2 %copy-start.9 = (f32[512]{0:T(512)S(1)}, f32[512]{0:T(512)}, u32[]{:S(2)}) copy-start(f32[512]{0:T(512)} %param.15) | copy-start | bytes 6148
  16.5 1.3 copy-start.10
  51.2 10.8 %copy-start.5 = (f32[1024,51]{0,1:T(8,128)S(1)}, f32[1024,51]{0,1:T(8,128)}, u32[]{:S(2)}) copy-start(f32[1024,51]{0,1:T(8,128)} %param.22) | copy-start | bytes 626692
  51.2 10.8 %copy-start.4 = (s32[1024,51]{0,1:T(8,128)S(1)}, s32[1024,51]{0,1:T(8,128)}, u32[]{:S(2)}) copy-start(s32[1024,51]{0,1:T(8,128)} %param.21) | copy-start | bytes 626692
  61.7 5.0 %copy-start.6 = (f32[1024]{0:T(1024)S(1)}, f32[1024]{0:T(1024)}, u32[]{:S(2)}) copy-start(f32[1024]{0:T(1024)} %param.23) | copy-start | bytes 12292
  70.1 3.9 %copy-start.3 = (bf16[1024,918]{0,1:T(8,128)(2,1)S(1)}, bf16[1024,918]{0,1:T(8,128)(2,1)}, u32[]{:S(2)}) copy-start(bf16[1024,918]{0,1:T(8,128)(2,1)} %convert_element_type.22) | copy-start | bytes 5640196
  70.1 3.9 %copy-start.11 = (f32[1024,512]{1,0:T(8,128)S(1)}, f32[1024,512]{1,0:T(8,128)}, u32[]{:S(2)}) copy-start(f32[1024,512]{1,0:T(8,128)} %copy-done.10) | copy-start | bytes 6291460
  268.0 6.5 %copy-start.2 = (f32[512,918]{0,1:T(8,128)S(1)}, f32[512,918]{0,1:T(8,128)}, u32[]{:S(2)}) copy-start(f32[512,918]{0,1:T(8,128)} %get-tuple-element.30) | copy-start | bytes 5640196
  268.0 7.7 %copy-start.1 = (bf16[512,3136]{0,1:T(8,128)(2,1)S(1)}, bf16[512,3136]{0,1:T(8,128)(2,1)}, u32[]{:S(2)}) copy-start(bf16[512,3136]{0,1:T(8,128)(2,1)} %param.14) | copy-start | bytes 9633796
Sparse Core Ops, SparseCore 0:
  84.8 183.0 all-reduce.3
where the time goes:
time: 285 us; the launch traced here: 284 us
  waiting for transfers between devices  94.7 us (33%)
  blocking collectives  84.8 us (30%)
  local copies, waits for them, and re-layouts  51.5 us (18%)
  matrix products  23.4 us (8%)
  between operations  16.7 us (6%)
  other arithmetic  12.5 us (4%)
    psum x1, waiting for transfers between devices, on_device(): grad_w1 = lax.psum(local_w1, 'dp')  94.7 us
    pmax x1, blocking collectives, on_device(): top = lax.pmax(local_top, 'dp')  43.8 us
    psum x1, blocking collectives, on_device(): grad_b1, grad_w2, grad_b2 = lax.psum((local_b1, local_w2, local_b2), 'dp')  41 us
    unnamed x27, local copies, waits for them, and re-layouts  16.6 us
    reshape x2, local copies, waits for them, and re-layouts, forward_loss(): (jnp.dot(hidden, w_two, preferred_element_type=jnp.float32) + b_two).resh...  11.3 us
    gather x2, local copies, waits for them, and re-layouts, forward_loss(): jnp.take_along_axis(target_probs, next_action[:, None, None], axis=1)  10.7 us
    gather x1, local copies, waits for them, and re-layouts, forward_loss(): chosen = jnp.take_along_axis(logits, action[:, None, None], axis=1)[:, 0, :]  10.6 us
    dot_general x1, matrix products, on_device(): lax.dot_general(grad_pre, features, (((0,), (0,)), ((), ())), preferred_e...  8.19 us
  transfers between devices with their start and end apart: 1, of which 1 were waited for; matrix products, arithmetic and copies ran while one was open for 1% of the time, Pallas kernels for 0%

commit v1 on v0

--- a/solution.py
+++ b/solution.py
@@ -100,7 +100,9 @@
     local_w1 = lax.dot_general(
         grad_pre, features, (((0,), (0,)), ((), ())), preferred_element_type=jnp.float32
     )
-    grad_w1 = lax.psum(local_w1, "dp")
+    grad_w1 = local_w1
+    for hop in (1, 2, 4, 8, 16):
+        grad_w1 = grad_w1 + lax.ppermute(grad_w1, "dp", [(dev, dev ^ hop) for dev in range(32)])
     priorities = cross_ent / jnp.maximum(top, 1.0)
     mean_loss = loss_sum / total_rows
     return (grad_w1, grad_b1, grad_w2, grad_b2, mean_loss, priorities)

time: 285 us -> 928 us (3.26)
  waiting for transfers between devices: 94.7 us -> 454 us
  blocking collectives: 84.8 us -> 339 us
  other arithmetic: 12.5 us -> 39.3 us
    ppermute x0 -> x5, waiting for transfers between devices: none -> 425 us  [on_device(): lax.ppermute(grad_w1, 'dp', [(dev, dev ^ hop) for dev in range(32)])]
    pmax x1, blocking collectives: 43.8 us -> 300 us  [on_device(): top = lax.pmax(local_top, 'dp')]
    psum x1, waiting for transfers between devices: 94.7 us -> 29.5 us  [on_device(): grad_b1, grad_w2, grad_b2 = lax.psum((local_b1, local_w2, local_b2), 'dp')]
    add x0 -> x5, other arithmetic: none -> 26.7 us  [on_device(): grad_w1 + lax.ppermute(grad_w1, 'dp', [(dev, dev ^ hop) for dev in range(...]
  transfers between devices with their start and end apart: 1 -> 6, of which waited for: 1 -> 5; matrix products, arithmetic and copies ran while one was open for 1% -> 2% of each run, Pallas kernels for 0% -> 0%
where the time goes in v1:
time: 928 us; the launch traced here: 927 us
  waiting for transfers between devices  454 us (49%)
  blocking collectives  339 us (37%)
  local copies, waits for them, and re-layouts  46.6 us (5%)
  other arithmetic  39.3 us (4%)
  matrix products  22.6 us (2%)
  between operations  16.7 us (2%)
    ppermute x5, waiting for transfers between devices, on_device(): lax.ppermute(grad_w1, 'dp', [(dev, dev ^ hop) for dev in range(32)])  425 us
    pmax x1, blocking collectives, on_device(): top = lax.pmax(local_top, 'dp')  300 us
    psum x1, blocking collectives, on_device(): grad_b1, grad_w2, grad_b2 = lax.psum((local_b1, local_w2, local_b2), 'dp')  39.2 us
    psum x1, waiting for transfers between devices, on_device(): grad_b1, grad_w2, grad_b2 = lax.psum((local_b1, local_w2, local_b2), 'dp')  29.5 us
    add x5, other arithmetic, on_device(): grad_w1 + lax.ppermute(grad_w1, 'dp', [(dev, dev ^ hop) for dev in range(...  26.7 us
  transfers between devices with their start and end apart: 6, of which 5 were waited for; matrix products, arithmetic and copies ran while one was open for 2% of the time, Pallas kernels for 0%

profile of v1, /device:TPU:0, one launch (start us, length us, event | category | flops | bytes accessed | tf_op | source)
XLA Modules:
  0.0 927.4 jit_solution(18053354973743958729)
XLA Ops:
  9.6 1.0 broadcast_add_fusion
  10.6 5.9 fusion.16
  16.5 1.3 copy-done.9
  17.8 3.0 convolution_add_fusion
  20.8 3.9 reshape.118
  24.7 7.5 copy.39
  32.2 10.6 %gather_fusion = f32[1024,51]{1,0:T(8,128)S(1)} fusion(f32[1024,18,51]{2,0,1:T(8,128)} %copy.39, s32[1024]{0:T(1024)S(1)} %bitcast.54), kind=kCustom, calls=%fused_computation.clone | custom fusion | bytes 425984 | tf_op jit(solution)/shard_map/jit(take_along_axis)/gather | solution.py:33
  43.7 7.5 copy.40
  51.2 10.5 %gather_fusion.1 = f32[1024,51]{1,0:T(8,128)S(1)} fusion(f32[1024,18,51]{2,0,1:T(8,128)} %copy.40, s32[1024]{0:T(1024)S(1)} %bitcast.53), kind=kCustom, calls=%fused_computation.1.clone | custom fusion | bytes 425984 | tf_op jit(solution)/shard_map/jit(take_along_axis)/gather | solution.py:35
  62.0 4.5 fusion.1
  66.7 1.1 fusion.3
  68.3 1.8 convert_element_type.22
  70.1 3.8 convert_reduce_fusion.1
  73.9 5.9 fusion.17
  80.4 10.1 %collective-permute-done = f32[512,3136]{0,1:T(8,128)} collective-permute-done((f32[512,3136]{0,1:T(8,128)S(1)}, f32[512,3136]{0,1:T(8,128)}, u32[]{:S(2)}, u32[]{:S(2)}) %collective-permute-start) | collective-permute-done | bytes 6422560 | tf_op jit(solution)/shard_map/ppermute | solution.py:105
  90.5 4.4 add.62
  94.9 2.9 collective-permute-start.1
  97.8 138.7 %collective-permute-done.1 = f32[512,3136]{0,1:T(8,128)} collective-permute-done((f32[512,3136]{0,1:T(8,128)S(1)}, f32[512,3136]{0,1:T(8,128)}, u32[]{:S(2)}, u32[]{:S(2)}) %collective-permute-start.1) | collective-permute-done | bytes 6422560 | tf_op jit(solution)/shard_map/ppermute | solution.py:105
  236.5 4.4 add.63
  240.9 1.7 collective-permute-start.2
  242.7 138.2 %collective-permute-done.2 = f32[512,3136]{0,1:T(8,128)} collective-permute-done((f32[512,3136]{0,1:T(8,128)S(1)}, f32[512,3136]{0,1:T(8,128)}, u32[]{:S(2)}, u32[]{:S(2)}) %collective-permute-start.2) | collective-permute-done | bytes 6422560 | tf_op jit(solution)/shard_map/ppermute | solution.py:105
  380.9 4.4 add.64
  385.3 1.5 collective-permute-start.3
  386.9 137.5 %collective-permute-done.3 = f32[512,3136]{0,1:T(8,128)S(1)} collective-permute-done((f32[512,3136]{0,1:T(8,128)S(1)}, f32[512,3136]{0,1:T(8,128)S(1)}, u32[]{:S(2)}, u32[]{:S(2)}) %collective-permute-start.3) | collective-permute-done | bytes 6422560 | tf_op jit(solution)/shard_map/ppermute | solution.py:105
  524.3 4.3 add.65
  528.7 2.3 collective-permute-start.4
  530.9 4.0 fusion.5
  536.2 299.9 %pmax.7 = f32[]{:T(128)} all-reduce(f32[]{:T(128)} %get-tuple-element.9), channel_id=1, replica_groups=mesh['dp'=32] {'dp'}, use_global_device_ids=true, to_apply=%region_13.15 | all-reduce | flops 1 | bytes 8 | tf_op jit(solution)/shard_map/pmax | solution.py:93
  837.4 39.2 %all-reduce = (f32[512]{0:T(512)}, f32[918]{0:T(1024)}, f32[]{:T(128)}) all-reduce(f32[512]{0:T(512)S(1)} %get-tuple-element.22, f32[918]{0:T(1024)S(1)} %reduce_sum.74, f32[]{:T(128)} %get-tuple-element.10), channel_id=1, replica_groups=mesh['dp'=32] {'dp'}, use_global_device_ids=true, to_apply=%region_5.7 | all-reduce | flops 1431 | bytes 11448 | tf_op jit(solution)/shard_map/psum | solution.py:99
  877.8 9.2 add.66
  887.0 29.5 %all-reduce.3.cloned.1.call-done = f32[512,918]{0,1:T(8,128)} async-done(((f32[512,918]{0,1:T(8,128)}), f32[512,918]{0,1:T(8,128)}) %all-reduce.3.cloned.1.call-update) | async-done | bytes 1880080 | tf_op jit(solution)/shard_map/psum | solution.py:99
  916.5 2.9 copy.46
  (42 shorter events, 7.4 us)
Async XLA Ops:
  7.2 3.4 copy-start
  7.2 909.3 %all-reduce.3.cloned.1.call-start = ((), (), s32[]{:S(2)}) async-start(), calls=%async_computation | async-start | bytes 3768320 | tf_op jit(solution)/shard_map/psum | solution.py:99
  10.5 7.3 copy-start.6
  10.6 7.3 copy-start.7
  10.6 7.2 copy-start.8
  16.5 1.3 copy-start.9
  51.2 10.8 %copy-start.4 = (f32[1024,51]{0,1:T(8,128)S(1)}, f32[1024,51]{0,1:T(8,128)}, u32[]{:S(2)}) copy-start(f32[1024,51]{0,1:T(8,128)} %param.22) | copy-start | bytes 626692
  51.2 10.8 %copy-start.3 = (s32[1024,51]{0,1:T(8,128)S(1)}, s32[1024,51]{0,1:T(8,128)}, u32[]{:S(2)}) copy-start(s32[1024,51]{0,1:T(8,128)} %param.21) | copy-start | bytes 626692
  51.2 15.5 %copy-start.5 = (f32[1024]{0:T(1024)S(1)}, f32[1024]{0:T(1024)}, u32[]{:S(2)}) copy-start(f32[1024]{0:T(1024)} %param.23) | copy-start | bytes 12292
  79.8 10.6 %collective-permute-start = (f32[512,3136]{0,1:T(8,128)S(1)}, f32[512,3136]{0,1:T(8,128)}, u32[]{:S(2)}, u32[]{:S(2)}) collective-permute-start(f32[512,3136]{0,1:T(8,128)S(1)} %fusion.17), channel_id=1, source_target_pairs={{0,1},{1,0},{2,3},{3,2},{4,5},{5,4},{6,7},{7,6},{8,9},{9,8},{10,11... | collective-permute-start | bytes 19267592 | tf_op jit(solution)/shard_map/ppermute | solution.py:105
  94.9 141.7 %collective-permute-start.1 = (f32[512,3136]{0,1:T(8,128)S(1)}, f32[512,3136]{0,1:T(8,128)}, u32[]{:S(2)}, u32[]{:S(2)}) collective-permute-start(f32[512,3136]{0,1:T(8,128)S(1)} %add.62), channel_id=1, source_target_pairs={{0,2},{1,3},{2,0},{3,1},{4,6},{5,7},{6,4},{7,5},{8,10},{9,11},{10,... | collective-permute-start | bytes 19267592 | tf_op jit(solution)/shard_map/ppermute | solution.py:105
  240.9 140.0 %collective-permute-start.2 = (f32[512,3136]{0,1:T(8,128)S(1)}, f32[512,3136]{0,1:T(8,128)}, u32[]{:S(2)}, u32[]{:S(2)}) collective-permute-start(f32[512,3136]{0,1:T(8,128)S(1)} %add.63), channel_id=1, source_target_pairs={{0,4},{1,5},{2,6},{3,7},{4,0},{5,1},{6,2},{7,3},{8,12},{9,13},{10,... | collective-permute-start | bytes 19267592 | tf_op jit(solution)/shard_map/ppermute | solution.py:105
  385.3 145.6 %copy-start.2 = (bf16[1024,918]{0,1:T(8,128)(2,1)S(1)}, bf16[1024,918]{0,1:T(8,128)(2,1)}, u32[]{:S(2)}) copy-start(bf16[1024,918]{0,1:T(8,128)(2,1)} %convert_element_type.22) | copy-start | bytes 5640196
  385.3 139.0 %collective-permute-start.3 = (f32[512,3136]{0,1:T(8,128)S(1)}, f32[512,3136]{0,1:T(8,128)S(1)}, u32[]{:S(2)}, u32[]{:S(2)}) collective-permute-start(f32[512,3136]{0,1:T(8,128)S(1)} %add.64), channel_id=1, source_target_pairs={{0,8},{1,9},{2,10},{3,11},{4,12},{5,13},{6,14},{7,15},{8,0},{9,1},... | collective-permute-start | bytes 19267592 | tf_op jit(solution)/shard_map/ppermute | solution.py:105
  528.7 349.2 %collective-permute-start.4 = (f32[512,3136]{0,1:T(8,128)}, f32[512,3136]{0,1:T(8,128)}, u32[]{:S(2)}, u32[]{:S(2)}) collective-permute-start(f32[512,3136]{0,1:T(8,128)} %add.65), channel_id=1, source_target_pairs={{0,16},{1,17},{2,18},{3,19},{4,20},{5,21},{6,22},{7,23},{8,24},{9,... | collective-permute-start | bytes 19267592 | tf_op jit(solution)/shard_map/ppermute | solution.py:105
  877.8 41.6 %copy-start.1 = (bf16[512,3136]{0,1:T(8,128)(2,1)S(1)}, bf16[512,3136]{0,1:T(8,128)(2,1)}, u32[]{:S(2)}) copy-start(bf16[512,3136]{0,1:T(8,128)(2,1)} %param.14) | copy-start | bytes 9633796
Sparse Core Ops, SparseCore 0:
  535.1 381.3 all-reduce.2
